TPU v7x, 32 devices: a whole 2x2x4 slice. The times are simulated.
32 devices in a mesh: replica: 4 (over x, core), fsdp: 8 (over z, y).
Axes of the slice: x: 2, y: 2, z: 4, core: 2. Of those that a mesh axis runs over, the one named last changes fastest.
Arguments:
- anchor: float32 [1536, 1536], P('fsdp', 'replica'), may hold values from -0.15625 to 0.15625
- momentum: float32 [1536, 1536], P('fsdp', 'replica'), may hold values from -0.75 to 0.75
- change: float32 [4, 1536, 1536], P('replica', 'fsdp'), may hold values from -0.75 to 0.75
- adam_first: float32 [4, 1536, 1536], P('replica', 'fsdp'), may hold values from -4 to 4
- adam_second: float32 [4, 1536, 1536], P('replica', 'fsdp'), may hold values from 0.1 to 2
- attn_out: bfloat16 [4, 8192, 1536], P('replica', 'fsdp'), may hold values from -6 to 6
- grad_out: bfloat16 [4, 8192, 1536], P('replica', 'fsdp'), may hold values from -6 to 6
Outputs:
- new_anchor: float32 [1536, 1536], P('fsdp', 'replica')
- new_momentum: float32 [1536, 1536], P('fsdp', 'replica')
- new_local: float32 [4, 1536, 1536], P('replica', 'fsdp')
- new_first: float32 [4, 1536, 1536], P('replica', 'fsdp')
- new_second: float32 [4, 1536, 1536], P('replica', 'fsdp')
- input_grad: bfloat16 [4, 8192, 1536], P('replica', 'fsdp')
All inputs are finite; a program needn't handle non-finite values.
Results may differ from a plain program's by a relative error of at most 0.0049.
Values may be sent and summed in bfloat16 or wider, within the bound.
A program may use at most 128 MiB of HBM per device.

v0:
```python
import jax
import jax.numpy as jnp
from jax import lax
from jax.sharding import PartitionSpec as P

outer_rate = 0.7
outer_mu = 0.9
inner_rate = 0.005
beta_one = 0.9
beta_two = 0.95
decay_rate = 0.1
epsilon = 1e-08


def shards(anchor, momentum, change, adam_first, adam_second, attn_out, grad_out):
    groups = lax.axis_size("replica")
    step_change = change[0]
    summed = lax.psum_scatter(step_change, "replica", scatter_dimension=1, tiled=True)
    outer_grad = -summed / groups
    new_momentum = outer_mu * momentum + outer_grad
    new_anchor = anchor - outer_rate * (outer_grad + outer_mu * new_momentum)
    anchor_next = lax.all_gather(new_anchor, "replica", axis=1, tiled=True)
    weights = anchor_next.astype(jnp.bfloat16)
    inputs = attn_out[0]
    cotangent = grad_out[0]
    grad_scale = (inputs.shape[0] * lax.axis_size("fsdp")) ** (-0.5)
    gradient = lax.psum_scatter(
        lax.dot_general(
            inputs, cotangent, (((0,), (0,)), ((), ())), preferred_element_type=jnp.float32
        ),
        "fsdp",
        scatter_dimension=0,
        tiled=True,
    )
    input_grad = lax.dot_general(
        cotangent,
        lax.all_gather(weights, "fsdp", axis=0, tiled=True),
        (((1,), (1,)), ((), ())),
        preferred_element_type=jnp.float32,
    ).astype(jnp.bfloat16)
    gradient = gradient * grad_scale
    first_next = beta_one * adam_first[0] + (1.0 - beta_one) * gradient
    second_next = beta_two * adam_second[0] + (1.0 - beta_two) * gradient * gradient
    local = anchor_next - inner_rate * (
        first_next / (jnp.sqrt(second_next) + epsilon) + decay_rate * anchor_next
    )
    return (
        new_anchor,
        new_momentum,
        local[None],
        first_next[None],
        second_next[None],
        input_grad[None],
    )


def solution(mesh):
    in_specs = (
        P("fsdp", "replica"),
        P("fsdp", "replica"),
        P("replica", "fsdp", None),
        P("replica", "fsdp", None),
        P("replica", "fsdp", None),
        P("replica", "fsdp", None),
        P("replica", "fsdp", None),
    )
    out_specs = (
        P("fsdp", "replica"),
        P("fsdp", "replica"),
        P("replica", "fsdp", None),
        P("replica", "fsdp", None),
        P("replica", "fsdp", None),
        P("replica", "fsdp", None),
    )
    return jax.shard_map(shards, mesh=mesh, in_specs=in_specs, out_specs=out_specs, check_vma=False)
```

profile of v0, /device:TPU:0, one launch (start us, length us, event | category | flops | bytes accessed | tf_op | source)
XLA Modules:
  0.0 318.5 jit_solution(14753706223368449582)
XLA Ops:
  8.0 0.0 copy-start
  8.0 0.0 copy-start.1
  8.0 0.0 reduce-scatter.3.cloned.1.call-start
  8.1 0.7 reduce-scatter.3.cloned.1.call-update
  8.8 0.0 all-gather.3.cloned.1.call-start
  8.8 31.0 %reduce-scatter.3.cloned.1.call-done = f32[192,384]{1,0:T(8,128)} async-done(((f32[192,1536]{1,0:T(8,128)}), f32[192,384]{1,0:T(8,128)}) %reduce-scatter.3.cloned.1.call-update) | async-done | bytes 294928 | tf_op jit(solution)/shard_map/reduce_scatter | solution.py:18
  39.8 0.0 copy-done.1
  39.8 1.9 multiply_subtract_fusion
  41.7 0.0 all-gather.3.cloned.1.call-update
  41.7 0.0 reduce-scatter.5.cloned.1.call-start
  41.8 0.0 copy-done
  41.8 9.7 %fusion.2 = f32[1536,1536]{1,0:T(8,128)} fusion(bf16[1,1024,1536]{2,1,0:T(8,128)(2,1)S(1)} %copy-done, bf16[1,1024,1536]{2,1,0:T(8,128)(2,1)} %param.12), kind=kOutput, calls=%fused_computation.3 | convolution fusion | flops 4831838208 | bytes 15728640 | tf_op jit(solution)/shard_map/dot_general | solution.py:28
  51.5 0.0 reduce-scatter.5.cloned.1.call-update
  51.5 0.0 all-gather.5.cloned.1.call-start
  51.6 7.8 %all-gather.3.cloned.1.call-done = f32[192,1536]{1,0:T(8,128)} async-done(((f32[192,384]{1,0:T(8,128)}), f32[192,1536]{1,0:T(8,128)}) %all-gather.3.cloned.1.call-update) | async-done | bytes 1179664 | tf_op jit(solution)/shard_map/all_gather | solution.py:22
  59.4 154.3 %reduce-scatter.5.cloned.1.call-done = f32[192,1536]{1,0:T(8,128)} async-done(((f32[1536,1536]{1,0:T(8,128)}), f32[192,1536]{1,0:T(8,128)}) %reduce-scatter.5.cloned.1.call-update) | async-done | bytes 1179664 | tf_op jit(solution)/shard_map/reduce_scatter | solution.py:27
  213.7 5.5 %fusion.6 = (f32[1,192,1536]{2,1,0:T(8,128)}, f32[1,192,1536]{2,1,0:T(8,128)}, f32[1,192,1536]{2,1,0:T(8,128)}, bf16[192,1536]{1,0:T(8,128)(2,1)}) fusion(f32[192,1536]{1,0:T(8,128)} %reduce-scatter.5.cloned.1.call-done, f32[1,192,1536]{2,1,0:T(8,128)} %param.11, f32[192,1536]{1,0:T(8,128)} %all-gather.3.cloned.1.call-done, f32[1,192,1536]{2,1,0:T(8,128)} %param.10), kind=kLoop, calls=%fused_computation.13 | loop fusion | flops 4423680 | bytes 8847360 | tf_op jit(solution)/shard_map/broadcast_in_dim | solution.py:52
  219.2 0.0 all-gather.5.cloned.1.call-update
  219.2 78.3 %all-gather.5.cloned.1.call-done = bf16[1536,1536]{1,0:T(8,128)(2,1)} async-done(((bf16[192,1536]{1,0:T(8,128)(2,1)}), bf16[1536,1536]{1,0:T(8,128)(2,1)}) %all-gather.5.cloned.1.call-update) | async-done | bytes 4718608 | tf_op jit(solution)/shard_map/all_gather | solution.py:37
  297.5 8.9 %fusion = bf16[1,1024,1536]{1,2,0:T(8,128)(2,1)} fusion(bf16[1536,1536]{1,0:T(8,128)(2,1)} %all-gather.5.cloned.1.call-done, bf16[1,1024,1536]{2,1,0:T(8,128)(2,1)S(1)} %copy-done), kind=kOutput, calls=%fused_computation.1 | convolution fusion | flops 4833411072 | bytes 11010048 | tf_op jit(solution)/shard_map/dot_general | solution.py:35
  306.4 4.6 %copy.13 = bf16[1,1024,1536]{2,1,0:T(8,128)(2,1)} copy(bf16[1,1024,1536]{1,2,0:T(8,128)(2,1)} %fusion) | data formatting | bytes 6291456
Async XLA Ops:
  8.0 33.8 %copy-start = (bf16[1,1024,1536]{2,1,0:T(8,128)(2,1)S(1)}, bf16[1,1024,1536]{2,1,0:T(8,128)(2,1)}, u32[]{:S(2)}) copy-start(bf16[1,1024,1536]{2,1,0:T(8,128)(2,1)} %param.13) | copy-start | bytes 9437188
  8.0 31.7 %copy-start.1 = (f32[192,384]{1,0:T(8,128)S(1)}, f32[192,384]{1,0:T(8,128)}, u32[]{:S(2)}) copy-start(f32[192,384]{1,0:T(8,128)} %param.7) | copy-start | bytes 884740
  8.0 31.7 %reduce-scatter.3.cloned.1.call-start = ((), (), s32[]{:S(2)}) async-start(), calls=%async_computation.2 | async-start | bytes 1474560 | tf_op jit(solution)/shard_map/reduce_scatter | solution.py:18
  8.8 50.6 %all-gather.3.cloned.1.call-start = ((), (), s32[]{:S(2)}) async-start(), calls=%async_computation.3 | async-start | bytes 1474560 | tf_op jit(solution)/shard_map/all_gather | solution.py:22
  41.7 171.9 %reduce-scatter.5.cloned.1.call-start = ((), (), s32[]{:S(2)}) async-start(), calls=%async_computation.4 | async-start | bytes 10616832 | tf_op jit(solution)/shard_map/reduce_scatter | solution.py:27
  51.5 246.0 %all-gather.5.cloned.1.call-start = ((), (), s32[]{:S(2)}) async-start(), calls=%async_computation.5 | async-start | bytes 5308416 | tf_op jit(solution)/shard_map/all_gather | solution.py:37
Sparse Core Ops, SparseCore 0:
  11.4 28.3 reduce-scatter.2
  41.9 17.4 all-gather.2
Sparse Core Ops, SparseCore 1:
  51.6 162.0 reduce-scatter.4
  219.3 78.2 all-gather.4
where the time goes:
time: 319 us; the launch traced here: 318 us
  waiting for transfers between devices  272 us (85%)
  matrix products  18.6 us (6%)
  between operations  15.5 us (5%)
  other arithmetic  7.45 us (2%)
  local copies, waits for them, and re-layouts  4.64 us (1%)
    reduce_scatter x1, waiting for transfers between devices, shards(): lax.psum_scatter(lax.dot_general(inputs, cotangent, (((0,), (0,)), ((), (...  154 us
    all_gather x1, waiting for transfers between devices, shards(): lax.all_gather(weights, 'fsdp', axis=0, tiled=True)  78.3 us
    reduce_scatter x1, waiting for transfers between devices, shards(): lax.psum_scatter(step_change, 'replica', scatter_dimension=1, tiled=True)  31 us
    dot_general x1, matrix products, shards(): lax.dot_general(inputs, cotangent, (((0,), (0,)), ((), ())), preferred_el...  9.72 us
    dot_general x1, matrix products, shards(): lax.dot_general(cotangent, lax.all_gather(weights, 'fsdp', axis=0, tiled=...  8.91 us
    all_gather x1, waiting for transfers between devices, shards(): anchor_next = lax.all_gather(new_anchor, 'replica', axis=1, tiled=True)  7.79 us
  transfers between devices with their start and end apart: 4, of which 4 were waited for; matrix products, arithmetic and copies ran while one was open for 3% of the time, Pallas kernels for 0%

commit v1 on v0

v1 whole, which is shorter than its diff:
```python
import functools

import jax
import jax.numpy as jnp
from jax import lax
from jax.experimental import pallas as pl
from jax.experimental.pallas import tpu as pltpu
from jax.sharding import PartitionSpec as P

outer_rate = 0.7
outer_mu = 0.9
inner_rate = 0.005
beta_one = 0.9
beta_two = 0.95
decay_rate = 0.1
epsilon = 1e-08

MESH = pl.DeviceIdType.MESH
f32 = jnp.float32
bf16 = jnp.bfloat16


def adam(anchor_next, first, second, gradient):
    first_next = beta_one * first + (1.0 - beta_one) * gradient
    second_next = beta_two * second + (1.0 - beta_two) * gradient * gradient
    local = anchor_next - inner_rate * (
        first_next / (jnp.sqrt(second_next) + epsilon) + decay_rate * anchor_next
    )
    return local, first_next, second_next


def outer_step(anchor, momentum, summed, groups):
    outer_grad = -summed / groups
    new_momentum = outer_mu * momentum + outer_grad
    new_anchor = anchor - outer_rate * (outer_grad + outer_mu * new_momentum)
    return new_anchor, new_momentum


def plain_shards(anchor, momentum, change, adam_first, adam_second, attn_out, grad_out):
    groups = lax.axis_size("replica")
    summed = lax.psum_scatter(change[0], "replica", scatter_dimension=1, tiled=True)
    new_anchor, new_momentum = outer_step(anchor, momentum, summed, groups)
    anchor_next = lax.all_gather(new_anchor, "replica", axis=1, tiled=True)
    inputs, cotangent = attn_out[0], grad_out[0]
    grad_scale = (inputs.shape[0] * lax.axis_size("fsdp")) ** (-0.5)
    gradient = grad_scale * lax.psum_scatter(
        lax.dot_general(inputs, cotangent, (((0,), (0,)), ((), ())), preferred_element_type=f32),
        "fsdp",
        scatter_dimension=0,
        tiled=True,
    )
    input_grad = lax.dot_general(
        cotangent,
        lax.all_gather(anchor_next.astype(bf16), "fsdp", axis=0, tiled=True),
        (((1,), (1,)), ((), ())),
        preferred_element_type=f32,
    ).astype(bf16)
    local, first, second = adam(anchor_next, adam_first[0], adam_second[0], gradient)
    return new_anchor, new_momentum, local[None], first[None], second[None], input_grad[None]


def kernel(
    depth, groups, scale,
    anchor_hbm, momentum_hbm, change_hbm, attn_hbm, cot_hbm,
    summed_ref, row_ref, grad_ref, back_hbm,
    anchor, momentum, change, attn, cot, flipped,
    part, got, own, psend, ry, zsend, chain, weights, back,
    local_sem, back_sem, part_s, part_r, py_s, py_r, ch_s, ch_r,
    az_s, az_r, ay_s, ay_r, ax_s, ax_r, as_s, as_r,
):
    r = lax.axis_index("replica")
    f = lax.axis_index("fsdp")
    x, core = r // 2, r % 2
    z, y = f // 2, f % 2
    rows, width = change.shape
    cols = width // groups
    pair = 2 * rows
    flip_y = {"replica": r, "fsdp": z * 2 + (1 - y)}
    flip_x = {"replica": (1 - x) * 2 + core, "fsdp": f}
    sibling = {"replica": x * 2 + (1 - core), "fsdp": f}

    def along_z(where):
        return {"replica": r, "fsdp": where * 2 + y}

    loads = []
    for i, (src, dst) in enumerate((
        (change_hbm, change), (anchor_hbm, anchor), (momentum_hbm, momentum),
        (attn_hbm, attn), (cot_hbm, cot),
    )):
        loads.append(pltpu.make_async_copy(src, dst, local_sem.at[i]))
        loads[-1].start()

    barrier = pltpu.get_barrier_semaphore()
    for k in range(1, groups):
        pl.semaphore_signal(
            barrier, inc=1, device_id={"replica": (r + k) % groups, "fsdp": f}, device_id_type=MESH
        )
    for k in range(1, depth):
        pl.semaphore_signal(barrier, inc=1, device_id=along_z((z + k) % depth), device_id_type=MESH)
    pl.semaphore_signal(barrier, inc=1, device_id=flip_y, device_id_type=MESH)

    def remote(src, dst, send, recv, device):
        return pltpu.make_async_remote_copy(
            src_ref=src, dst_ref=dst, send_sem=send, recv_sem=recv,
            device_id=device, device_id_type=MESH,
        )

    loads[0].wait()
    for k in range(groups):
        at = pl.multiple_of(((r + k) % groups) * cols, 128)
        part[k] = change[:, pl.ds(at, cols)].astype(bf16)
    pl.semaphore_wait(barrier, groups + depth - 1)
    parts = []
    for k in range(1, groups):
        parts.append(remote(
            part.at[k], got.at[k - 1], part_s.at[k - 1], part_r.at[k - 1],
            {"replica": (r + k) % groups, "fsdp": f},
        ))
        parts[-1].start()

    def block_at(i):
        low = jnp.where(i < depth - 1 - z, depth - 1 - i, i - (depth - 1 - z))
        high = jnp.where(i < z, i, depth - 1 - (i - z))
        return jnp.where(z < depth // 2, low, high)

    loads[3].wait()
    loads[4].wait()
    tile = 512 if width % 512 == 0 else 128
    y_copies = [
        remote(psend.at[i], ry.at[i], py_s.at[i], py_r.at[i], flip_y) for i in range(depth)
    ]

    def multiply(i):
        at = pl.multiple_of(block_at(i) * pair, 128)
        flipped[...] = attn[:, pl.ds(at, pair)].T

        def columns(c, carry):
            there = pl.ds(pl.multiple_of(c * tile, 128), tile)
            product = jnp.dot(flipped[...], cot[:, there], preferred_element_type=f32)
            upper, lower = product[:rows], product[rows:]
            own[i, :, there] = jnp.where(y == 0, upper, lower)
            psend[i, :, there] = jnp.where(y == 0, lower, upper).astype(bf16)
            return carry

        lax.fori_loop(0, width // tile, columns, 0)

    for i in range(depth):
        multiply(i)
        if i < 2:
            y_copies[i].start()

    loads[1].wait()
    loads[2].wait()
    for k in range(1, groups):
        parts[k - 1].wait_recv()
    mine = pl.ds(pl.multiple_of(r * cols, 128), cols)
    total = change[:, mine]
    for k in range(1, groups):
        total = total + got[k - 1].astype(f32)
    summed_ref[...] = total
    weights[f, :, mine] = outer_step(anchor[...], momentum[...], total, groups)[0].astype(bf16)

    def shard(zs, ys, xs, cs):
        at = pl.multiple_of((xs * 2 + cs) * cols, 128)
        return weights.at[zs * 2 + ys, :, pl.ds(at, cols)]

    def forward(kind, sends, recvs, index, where, device):
        ref = shard(*where)
        copy = remote(ref, ref, sends.at[index], recvs.at[index], device)
        copy.start()
        return copy

    def arrived(recvs, sends, index, where):
        ref = shard(*where)
        remote(ref, ref, sends.at[index], recvs.at[index], sibling).wait_recv()

    pending = []
    here = (z, y, x, core)
    for k in range(1, depth):
        pending.append(forward("z", az_s, az_r, k - 1, here, along_z((z + k) % depth)))
    pending.append(forward("y", ay_s, ay_r, 0, here, flip_y))
    pending.append(forward("x", ax_s, ax_r, 0, here, flip_x))
    pending.append(forward("s", as_s, as_r, 0, here, sibling))
    for k in range(1, depth):
        where = ((z + depth - k) % depth, y, x, core)
        arrived(az_r, az_s, k - 1, where)
        pending.append(forward("y", ay_s, ay_r, k, where, flip_y))
        pending.append(forward("x", ax_s, ax_r, k, where, flip_x))
        pending.append(forward("s", as_s, as_r, k, where, sibling))
    for i in range(2, depth):
        y_copies[i].start()

    lines = 16

    def reduce_step(i):
        y_copies[i].wait_recv()
        dest = block_at(i)
        up = dest > z
        slot = dest + jnp.where(up, 0, depth)
        follows = jnp.where(up, z > 0, z < depth - 1)
        copy = remote(
            zsend.at[i], chain.at[slot], ch_s.at[i], ch_r.at[slot],
            along_z(z + jnp.where(up, 1, -1)),
        )

        @pl.when(follows)
        def _():
            copy.wait_recv()

            def add(j, carry):
                there = pl.ds(pl.multiple_of(j * lines, lines), lines)
                zsend[i, there] = (
                    own[i, there] + ry[i, there].astype(f32) + chain[slot, there].astype(f32)
                ).astype(bf16)
                return carry

            lax.fori_loop(0, rows // lines, add, 0)

        @pl.when(jnp.logical_not(follows))
        def _():
            def add(j, carry):
                there = pl.ds(pl.multiple_of(j * lines, lines), lines)
                zsend[i, there] = (own[i, there] + ry[i, there].astype(f32)).astype(bf16)
                return carry

            lax.fori_loop(0, rows // lines, add, 0)

        copy.start()
        return copy

    chains = [reduce_step(0)]
    for k in range(depth):
        where = ((z + depth - k) % depth, 1 - y, x, core)
        arrived(ay_r, ay_s, k, where)
        pending.append(forward("x", ax_s, ax_r, depth + k, where, flip_x))
        pending.append(forward("s", as_s, as_r, depth + k, where, sibling))
    for i in range(1, depth - 1):
        chains.append(reduce_step(i))
    for dy in range(2):
        for k in range(depth):
            where = ((z + depth - k) % depth, y + dy - 2 * y * dy, 1 - x, core)
            arrived(ax_r, ax_s, dy * depth + k, where)
            pending.append(forward("s", as_s, as_r, (2 + dy) * depth + k, where, sibling))
    for dx in range(2):
        for dy in range(2):
            for k in range(depth):
                where = (
                    (z + depth - k) % depth, y + dy - 2 * y * dy, x + dx - 2 * x * dx, 1 - core
                )
                arrived(as_r, as_s, (2 * dx + dy) * depth + k, where)
    row_ref[...] = weights[f]

    def back_copy(c):
        there = pl.ds(pl.multiple_of(c * pair, 128), pair)
        return pltpu.make_async_copy(back.at[:, there], back_hbm.at[:, there], back_sem.at[c])

    def back_step(c, carry):
        there = pl.ds(pl.multiple_of(c * pair, 128), pair)
        block = weights[pl.ds(2 * c, 2)].reshape(pair, width)
        back[:, there] = lax.dot_general(
            cot[...], block, (((1,), (1,)), ((), ())), preferred_element_type=f32
        ).astype(bf16)
        return carry

    for c in range(depth):
        back_step(c, 0)
        back_copy(c).start()

    last = depth - 1
    y_copies[last].wait_recv()
    grad_ref[...] = (own[last] + ry[last].astype(f32)) * scale
    for slot, follows in ((z, z > 0), (depth + z, z < depth - 1)):
        @pl.when(follows)
        def _():
            remote(
                zsend.at[0], chain.at[slot], ch_s.at[0], ch_r.at[slot], flip_y
            ).wait_recv()
            grad_ref[...] += chain[slot].astype(f32) * scale

    for copy in parts + y_copies + pending + chains:
        copy.wait_send()
    for c in range(depth):
        back_copy(c).wait()


def fused_shards(anchor, momentum, change, adam_first, adam_second, attn_out, grad_out):
    groups, devices = lax.axis_size("replica"), lax.axis_size("fsdp")
    depth = devices // 2
    rows, width = change.shape[1:]
    tokens = attn_out.shape[1]
    cols = width // groups
    scale = (tokens * devices) ** (-0.5)
    dma = pltpu.SemaphoreType.DMA
    vmem = pltpu.VMEM
    any_space = pl.BlockSpec(memory_space=pl.ANY)
    in_vmem = pl.BlockSpec(memory_space=pltpu.VMEM)
    summed, anchor_row, gradient, input_grad = pl.pallas_call(
        functools.partial(kernel, depth, groups, scale),
        out_shape=(
            jax.ShapeDtypeStruct((rows, cols), f32),
            jax.ShapeDtypeStruct((rows, width), bf16),
            jax.ShapeDtypeStruct((rows, width), f32),
            jax.ShapeDtypeStruct((tokens, width), bf16),
        ),
        in_specs=[any_space] * 5,
        out_specs=(in_vmem, in_vmem, in_vmem, any_space),
        scratch_shapes=[
            vmem((rows, cols), f32),
            vmem((rows, cols), f32),
            vmem((rows, width), f32),
            vmem((tokens, width), bf16),
            vmem((tokens, width), bf16),
            vmem((2 * rows, tokens), bf16),
            vmem((groups, rows, cols), bf16),
            vmem((groups - 1, rows, cols), bf16),
            vmem((depth, rows, width), f32),
            vmem((depth, rows, width), bf16),
            vmem((depth, rows, width), bf16),
            vmem((depth, rows, width), bf16),
            vmem((2 * depth, rows, width), bf16),
            vmem((devices, rows, width), bf16),
            vmem((tokens, width), bf16),
            dma((5,)), dma((depth,)),
            dma((groups - 1,)), dma((groups - 1,)),
            dma((depth,)), dma((depth,)),
            dma((depth,)), dma((2 * depth,)),
            dma((depth - 1,)), dma((depth - 1,)),
            dma((depth,)), dma((depth,)),
            dma((2 * depth,)), dma((2 * depth,)),
            dma((4 * depth,)), dma((4 * depth,)),
        ],
        compiler_params=pltpu.CompilerParams(
            collective_id=0, has_side_effects=True, vmem_limit_bytes=60 * 2**20
        ),
    )(anchor, momentum, change[0], attn_out[0], grad_out[0])
    new_anchor, new_momentum = outer_step(anchor, momentum, summed, groups)
    local, first, second = adam(anchor_row.astype(f32), adam_first[0], adam_second[0], gradient)
    return new_anchor, new_momentum, local[None], first[None], second[None], input_grad[None]


def shards(*arrays):
    groups, devices = lax.axis_size("replica"), lax.axis_size("fsdp")
    rows, width = arrays[2].shape[1:]
    fits = (
        groups == 4 and devices % 2 == 0 and devices >= 4 and rows % 32 == 0
        and (2 * rows) % 128 == 0 and width % (128 * groups) == 0
        and arrays[5].shape[1] * width <= 2**21
    )
    return (fused_shards if fits else plain_shards)(*arrays)


def solution(mesh):
    in_specs = (P("fsdp", "replica"),) * 2 + (P("replica", "fsdp", None),) * 5
    out_specs = (P("fsdp", "replica"),) * 2 + (P("replica", "fsdp", None),) * 4
    return jax.shard_map(shards, mesh=mesh, in_specs=in_specs, out_specs=out_specs, check_vma=False)
```

time: 319 us -> 85.4 us (0.27)
  waiting for transfers between devices: 272 us -> 0 us
  Pallas kernels: 0 us -> 76.7 us
  matrix products: 18.6 us -> 0 us
  between operations: 15.5 us -> 0.69 us
    reduce_scatter x2 -> x0, waiting for transfers between devices: 185 us -> none  [the longest x1 154 us: shards(): lax.psum_scatter(lax.dot_general(inputs, cotangent, (((0,), (0,)), ((), (...]
    all_gather x2 -> x0, waiting for transfers between devices: 86.1 us -> none  [the longest x1 78.3 us: shards(): lax.all_gather(weights, 'fsdp', axis=0, tiled=True)]
    pallas_call x0 -> x1, Pallas kernels: none -> 76.7 us  [fused_shards(): pl.pallas_call(functools.partial(kernel, depth, groups, scale), out_shape...]
    dot_general x2 -> x0, matrix products: 18.6 us -> none  [the longest x1 9.72 us: shards(): lax.dot_general(inputs, cotangent, (((0,), (0,)), ((), ())), preferred_el...]
  transfers between devices with their start and end apart: 4 -> 0, of which waited for: 4 -> 0; matrix products, arithmetic and copies ran while one was open for 3% -> 0% of each run, Pallas kernels for 0% -> 0%
where the time goes in v1:
time: 85.4 us; the launch traced here: 85.2 us
  Pallas kernels  76.7 us (90%)
  other arithmetic  6.14 us (7%)
  local copies, waits for them, and re-layouts  1.69 us (2%)
    pallas_call x1, Pallas kernels, fused_shards(): pl.pallas_call(functools.partial(kernel, depth, groups, scale), out_shape...  76.7 us
    broadcast_in_dim x1, other arithmetic, fused_shards(): second[None]  4.2 us
    sub x1, other arithmetic, outer_step(): new_anchor = anchor - outer_rate * (outer_grad + outer_mu * new_momentum)  1.94 us

profile of v1, /device:TPU:0, one launch (start us, length us, event | category | flops | bytes accessed | tf_op | source)
XLA Modules:
  0.0 85.2 jit_solution(10482047377194562195)
XLA Ops:
  0.6 0.0 copy-start.1
  0.6 0.0 copy-start.2
  0.7 0.0 copy-start.4
  0.7 76.7 %shard_map.118 = (f32[192,384]{1,0:T(8,128)}, bf16[192,1536]{1,0:T(8,128)(2,1)}, f32[192,1536]{1,0:T(8,128)}, bf16[1024,1536]{1,0:T(8,128)(2,1)}) custom-call(f32[192,384]{1,0:T(8,128)} %anchor_hbm.1, f32[192,384]{1,0:T(8,128)} %momentum_hbm.1, f32[192,1536]{1,0:T(8,128)} %bitcast.25, bf16[1024,1536]{1,0:T(8,128)(2,1)} %bitcast.23, bf16[1024,1536]{1,0:T(8,128)(2,1)} %bitcast.24), custom_call_target="tpu_custom_call" | custom-call | tf_op jit(solution)/shard_map/pallas_call | solution.py:297
  77.4 0.0 copy-start.3
  77.4 0.0 copy-done.1
  77.4 0.0 copy-done.2
  77.4 1.9 %multiply_subtract_fusion = (f32[192,384]{1,0:T(8,128)}, f32[192,384]{1,0:T(8,128)}) fusion(f32[192,384]{1,0:T(8,128)S(1)} %copy-done.1, f32[192,384]{1,0:T(8,128)} %get-tuple-element.10, f32[192,384]{1,0:T(8,128)S(1)} %copy-done.2), kind=kLoop, calls=%fused_computation.10 | loop fusion | flops 589824 | bytes 1474560 | tf_op jit(solution)/shard_map/sub | solution.py:35
  79.4 0.0 copy-done.4
  79.4 0.0 copy-done.3
  79.4 0.0 copy-start
  79.4 4.2 %fusion.5 = (f32[1,192,1536]{2,1,0:T(8,128)}, f32[1,192,1536]{2,1,0:T(8,128)}, f32[1,192,1536]{2,1,0:T(8,128)}) fusion(f32[192,1536]{1,0:T(8,128)} %get-tuple-element.12, f32[1,192,1536]{2,1,0:T(8,128)S(1)} %copy-done.3, f32[1,192,1536]{2,1,0:T(8,128)S(1)} %copy-done.4, bf16[192,1536]{1,0:T(8,128)(2,1)} %get-tuple-element.11), kind=kLoop, calls=%fused_computation.9 | loop fusion | flops 4128768 | bytes 7667712 | tf_op jit(solution)/shard_map/broadcast_in_dim | solution.py:338
  83.6 0.0 copy-done
  83.6 1.7 %copy.14 = bf16[1,1024,1536]{2,1,0:T(8,128)(2,1)} copy(bf16[1,1024,1536]{2,1,0:T(8,128)(2,1)S(1)} %bitcast.22) | data formatting | bytes 6291456
Async XLA Ops:
  0.6 76.8 %copy-start.1 = (f32[192,384]{1,0:T(8,128)S(1)}, f32[192,384]{1,0:T(8,128)}, u32[]{:S(2)}) copy-start(f32[192,384]{1,0:T(8,128)} %anchor_hbm.1) | copy-start | bytes 884740
  0.6 76.8 %copy-start.2 = (f32[192,384]{1,0:T(8,128)S(1)}, f32[192,384]{1,0:T(8,128)}, u32[]{:S(2)}) copy-start(f32[192,384]{1,0:T(8,128)} %momentum_hbm.1) | copy-start | bytes 884740
  0.7 78.7 %copy-start.4 = (f32[1,192,1536]{2,1,0:T(8,128)S(1)}, f32[1,192,1536]{2,1,0:T(8,128)}, u32[]{:S(2)}) copy-start(f32[1,192,1536]{2,1,0:T(8,128)} %param.10) | copy-start | bytes 3538948
  77.4 2.0 %copy-start.3 = (f32[1,192,1536]{2,1,0:T(8,128)S(1)}, f32[1,192,1536]{2,1,0:T(8,128)}, u32[]{:S(2)}) copy-start(f32[1,192,1536]{2,1,0:T(8,128)} %param.11) | copy-start | bytes 3538948
  79.4 4.2 %copy-start = (bf16[1024,1536]{1,0:T(8,128)(2,1)S(1)}, bf16[1024,1536]{1,0:T(8,128)(2,1)}, u32[]{:S(2)}) copy-start(bf16[1024,1536]{1,0:T(8,128)(2,1)} %get-tuple-element.13) | copy-start | bytes 9437188

commit v2 on v1

--- a/solution.py
+++ b/solution.py
@@ -65,7 +65,9 @@
     summed_ref, row_ref, grad_ref, back_hbm,
     anchor, momentum, change, attn, cot, flipped,
     part, got, own, psend, ry, zsend, chain, weights, back,
+    lead_own, lead_send, lead_chain, lead_out, lead_in,
     local_sem, back_sem, part_s, part_r, py_s, py_r, ch_s, ch_r,
+    lz_s, lz_r, ly_s, ly_r,
     az_s, az_r, ay_s, ay_r, ax_s, ax_r, as_s, as_r,
 ):
     r = lax.axis_index("replica")
@@ -123,31 +125,61 @@
         high = jnp.where(i < z, i, depth - 1 - (i - z))
         return jnp.where(z < depth // 2, low, high)
 
+    lead = lead_own.shape[2]
+    half = (width - lead) // 2
+    last = depth - 1
+    inner = jnp.logical_and(z > 0, z < last)
+
+    def y_copy(i, h):
+        there = pl.ds(pl.multiple_of(h * half, 128), half)
+        return remote(
+            psend.at[i, :, there], ry.at[i, :, there], py_s.at[2 * i + h], py_r.at[2 * i + h],
+            flip_y,
+        )
+
+    def route(i):
+        dest = block_at(i)
+        up = dest > z
+        return dest + jnp.where(up, 0, depth), along_z(z + jnp.where(up, 1, -1))
+
+    def lead_copy(i):
+        slot, device = route(i)
+        return remote(
+            lead_send.at[i], lead_chain.at[slot], lz_s.at[i], lz_r.at[slot], device
+        )
+
     loads[3].wait()
     loads[4].wait()
-    tile = 512 if width % 512 == 0 else 128
-    y_copies = [
-        remote(psend.at[i], ry.at[i], py_s.at[i], py_r.at[i], flip_y) for i in range(depth)
-    ]
-
-    def multiply(i):
+
+    def multiply(i, carry):
         at = pl.multiple_of(block_at(i) * pair, 128)
         flipped[...] = attn[:, pl.ds(at, pair)].T
 
-        def columns(c, carry):
-            there = pl.ds(pl.multiple_of(c * tile, 128), tile)
+        def columns(h, carry):
+            there = pl.ds(pl.multiple_of(lead + h * half, 128), half)
             product = jnp.dot(flipped[...], cot[:, there], preferred_element_type=f32)
             upper, lower = product[:rows], product[rows:]
-            own[i, :, there] = jnp.where(y == 0, upper, lower)
-            psend[i, :, there] = jnp.where(y == 0, lower, upper).astype(bf16)
+            here = pl.ds(pl.multiple_of(h * half, 128), half)
+            own[i, :, here] = jnp.where(y == 0, upper, lower)
+            psend[i, :, here] = jnp.where(y == 0, lower, upper).astype(bf16)
+
+            @pl.when(i < 2)
+            def _():
+                y_copy(i, h).start()
+
             return carry
 
-        lax.fori_loop(0, width // tile, columns, 0)
-
-    for i in range(depth):
-        multiply(i)
-        if i < 2:
-            y_copies[i].start()
+        lax.fori_loop(0, 2, columns, 0)
+        lead_own[i] = jnp.dot(flipped[...], cot[:, :lead], preferred_element_type=f32)
+
+        @pl.when(jnp.logical_and(jnp.logical_not(inner), i < last))
+        def _():
+            lead_send[i] = lead_own[i].astype(bf16)
+            lead_copy(i).start()
+
+        return carry
+
+    lax.fori_loop(0, depth, multiply, 0)
 
     loads[1].wait()
     loads[2].wait()
@@ -181,6 +213,19 @@
     pending.append(forward("y", ay_s, ay_r, 0, here, flip_y))
     pending.append(forward("x", ax_s, ax_r, 0, here, flip_x))
     pending.append(forward("s", as_s, as_r, 0, here, sibling))
+
+    @pl.when(inner)
+    def _():
+        def pass_on(i, carry):
+            slot, _ = route(i)
+            copy = lead_copy(i)
+            copy.wait_recv()
+            lead_send[i] = (lead_own[i] + lead_chain[slot].astype(f32)).astype(bf16)
+            copy.start()
+            return carry
+
+        lax.fori_loop(0, last, pass_on, 0)
+
     for k in range(1, depth):
         where = ((z + depth - k) % depth, y, x, core)
         arrived(az_r, az_s, k - 1, where)
@@ -188,22 +233,18 @@
         pending.append(forward("x", ax_s, ax_r, k, where, flip_x))
         pending.append(forward("s", as_s, as_r, k, where, sibling))
     for i in range(2, depth):
-        y_copies[i].start()
+        for h in range(2):
+            y_copy(i, h).start()
 
     lines = 16
 
     def reduce_step(i):
-        y_copies[i].wait_recv()
-        dest = block_at(i)
-        up = dest > z
-        slot = dest + jnp.where(up, 0, depth)
-        follows = jnp.where(up, z > 0, z < depth - 1)
-        copy = remote(
-            zsend.at[i], chain.at[slot], ch_s.at[i], ch_r.at[slot],
-            along_z(z + jnp.where(up, 1, -1)),
-        )
-
-        @pl.when(follows)
+        for h in range(2):
+            y_copy(i, h).wait_recv()
+        slot, device = route(i)
+        copy = remote(zsend.at[i], chain.at[slot], ch_s.at[i], ch_r.at[slot], device)
+
+        @pl.when(inner)
         def _():
             copy.wait_recv()
 
@@ -216,7 +257,7 @@
 
             lax.fori_loop(0, rows // lines, add, 0)
 
-        @pl.when(jnp.logical_not(follows))
+        @pl.when(jnp.logical_not(inner))
         def _():
             def add(j, carry):
                 there = pl.ds(pl.multiple_of(j * lines, lines), lines)
@@ -234,7 +275,17 @@
         arrived(ay_r, ay_s, k, where)
         pending.append(forward("x", ax_s, ax_r, depth + k, where, flip_x))
         pending.append(forward("s", as_s, as_r, depth + k, where, sibling))
-    for i in range(1, depth - 1):
+    for slot, follows in ((z, z > 0), (depth + z, z < last)):
+        @pl.when(follows)
+        def _():
+            remote(
+                lead_send.at[0], lead_chain.at[slot], lz_s.at[0], lz_r.at[slot], flip_y
+            ).wait_recv()
+            lead_own[last] += lead_chain[slot].astype(f32)
+    lead_out[...] = lead_own[last, pl.ds(pl.multiple_of((1 - y) * rows, 8), rows)].astype(bf16)
+    lead_swap = remote(lead_out, lead_in, ly_s.at[0], ly_r.at[0], flip_y)
+    lead_swap.start()
+    for i in range(1, last):
         chains.append(reduce_step(i))
     for dy in range(2):
         for k in range(depth):
@@ -260,27 +311,38 @@
         back[:, there] = lax.dot_general(
             cot[...], block, (((1,), (1,)), ((), ())), preferred_element_type=f32
         ).astype(bf16)
+        back_copy(c).start()
         return carry
 
-    for c in range(depth):
-        back_step(c, 0)
-        back_copy(c).start()
-
-    last = depth - 1
-    y_copies[last].wait_recv()
-    grad_ref[...] = (own[last] + ry[last].astype(f32)) * scale
-    for slot, follows in ((z, z > 0), (depth + z, z < depth - 1)):
+    lax.fori_loop(0, depth, back_step, 0)
+
+    lead_swap.wait_recv()
+    kept = lead_own[last, pl.ds(pl.multiple_of(y * rows, 8), rows)]
+    grad_ref[:, :lead] = (kept + lead_in[...].astype(f32)) * scale
+    for h in range(2):
+        y_copy(last, h).wait_recv()
+    grad_ref[:, lead:] = (own[last] + ry[last].astype(f32)) * scale
+    for slot, follows in ((z, z > 0), (depth + z, z < last)):
         @pl.when(follows)
         def _():
             remote(
                 zsend.at[0], chain.at[slot], ch_s.at[0], ch_r.at[slot], flip_y
             ).wait_recv()
-            grad_ref[...] += chain[slot].astype(f32) * scale
-
-    for copy in parts + y_copies + pending + chains:
+            grad_ref[:, lead:] += chain[slot].astype(f32) * scale
+
+    for copy in parts + pending + chains + [lead_swap]:
         copy.wait_send()
+    for i in range(depth):
+        for h in range(2):
+            y_copy(i, h).wait_send()
+    for i in range(last):
+        lead_copy(i).wait_send()
     for c in range(depth):
         back_copy(c).wait()
+
+
+def lead_columns(width):
+    return width // 6 // 128 * 128
 
 
 def fused_shards(anchor, momentum, change, adam_first, adam_second, attn_out, grad_out):
@@ -289,6 +351,8 @@
     rows, width = change.shape[1:]
     tokens = attn_out.shape[1]
     cols = width // groups
+    lead = lead_columns(width)
+    rest = width - lead
     scale = (tokens * devices) ** (-0.5)
     dma = pltpu.SemaphoreType.DMA
     vmem = pltpu.VMEM
@@ -313,17 +377,23 @@
             vmem((2 * rows, tokens), bf16),
             vmem((groups, rows, cols), bf16),
             vmem((groups - 1, rows, cols), bf16),
-            vmem((depth, rows, width), f32),
-            vmem((depth, rows, width), bf16),
-            vmem((depth, rows, width), bf16),
-            vmem((depth, rows, width), bf16),
-            vmem((2 * depth, rows, width), bf16),
+            vmem((depth, rows, rest), f32),
+            vmem((depth, rows, rest), bf16),
+            vmem((depth, rows, rest), bf16),
+            vmem((depth, rows, rest), bf16),
+            vmem((2 * depth, rows, rest), bf16),
             vmem((devices, rows, width), bf16),
             vmem((tokens, width), bf16),
+            vmem((depth, 2 * rows, lead), f32),
+            vmem((depth, 2 * rows, lead), bf16),
+            vmem((2 * depth, 2 * rows, lead), bf16),
+            vmem((rows, lead), bf16),
+            vmem((rows, lead), bf16),
             dma((5,)), dma((depth,)),
             dma((groups - 1,)), dma((groups - 1,)),
-            dma((depth,)), dma((depth,)),
+            dma((2 * depth,)), dma((2 * depth,)),
             dma((depth,)), dma((2 * depth,)),
+            dma((depth,)), dma((2 * depth,)), dma((1,)), dma((1,)),
             dma((depth - 1,)), dma((depth - 1,)),
             dma((depth,)), dma((depth,)),
             dma((2 * depth,)), dma((2 * depth,)),
@@ -344,6 +414,7 @@
     fits = (
         groups == 4 and devices % 2 == 0 and devices >= 4 and rows % 32 == 0
         and (2 * rows) % 128 == 0 and width % (128 * groups) == 0
+        and lead_columns(width) > 0 and (width - lead_columns(width)) % 256 == 0
         and arrays[5].shape[1] * width <= 2**21
     )
     return (fused_shards if fits else plain_shards)(*arrays)

time: 85.4 us -> 78.3 us (0.917); the launches traced: 85.2 us -> 77.1 us
  Pallas kernels: 76.7 us -> 68.6 us
    pallas_call x1, Pallas kernels: 76.7 us -> 68.6 us  [fused_shards(): pl.pallas_call(functools.partial(kernel, depth, groups, scale), out_shape...]
where the time goes in v2:
time: 78.3 us; the launch traced here: 77.1 us
  Pallas kernels  68.6 us (88%)
  other arithmetic  6.14 us (8%)
  local copies, waits for them, and re-layouts  1.69 us (2%)
    pallas_call x1, Pallas kernels, fused_shards(): pl.pallas_call(functools.partial(kernel, depth, groups, scale), out_shape...  68.6 us
    broadcast_in_dim x1, other arithmetic, fused_shards(): second[None]  4.2 us
    sub x1, other arithmetic, outer_step(): new_anchor = anchor - outer_rate * (outer_grad + outer_mu * new_momentum)  1.94 us
    unnamed x11, local copies, waits for them, and re-layouts  1.69 us

profile of v2, /device:TPU:0, one launch (start us, length us, event | category | flops | bytes accessed | tf_op | source)
XLA Modules:
  0.0 77.1 jit_solution(11521251748979423458)
XLA Ops:
  0.6 0.0 copy-start.1
  0.6 0.0 copy-start.2
  0.7 0.0 copy-start.4
  0.7 68.6 %shard_map.118 = (f32[192,384]{1,0:T(8,128)}, bf16[192,1536]{1,0:T(8,128)(2,1)}, f32[192,1536]{1,0:T(8,128)}, bf16[1024,1536]{1,0:T(8,128)(2,1)}) custom-call(f32[192,384]{1,0:T(8,128)} %anchor_hbm.1, f32[192,384]{1,0:T(8,128)} %momentum_hbm.1, f32[192,1536]{1,0:T(8,128)} %bitcast.25, bf16[1024,1536]{1,0:T(8,128)(2,1)} %bitcast.23, bf16[1024,1536]{1,0:T(8,128)(2,1)} %bitcast.24), custom_call_target="tpu_custom_call" | custom-call | tf_op jit(solution)/shard_map/pallas_call | solution.py:361
  69.2 0.0 copy-start.3
  69.2 0.0 copy-done.1
  69.3 0.0 copy-done.2
  69.3 1.9 %multiply_subtract_fusion = (f32[192,384]{1,0:T(8,128)}, f32[192,384]{1,0:T(8,128)}) fusion(f32[192,384]{1,0:T(8,128)S(1)} %copy-done.1, f32[192,384]{1,0:T(8,128)} %get-tuple-element.10, f32[192,384]{1,0:T(8,128)S(1)} %copy-done.2), kind=kLoop, calls=%fused_computation.10 | loop fusion | flops 589824 | bytes 1474560 | tf_op jit(solution)/shard_map/sub | solution.py:35
  71.2 0.0 copy-done.4
  71.2 0.0 copy-done.3
  71.2 0.0 copy-start
  71.2 4.2 %fusion.5 = (f32[1,192,1536]{2,1,0:T(8,128)}, f32[1,192,1536]{2,1,0:T(8,128)}, f32[1,192,1536]{2,1,0:T(8,128)}) fusion(f32[192,1536]{1,0:T(8,128)} %get-tuple-element.12, f32[1,192,1536]{2,1,0:T(8,128)S(1)} %copy-done.3, f32[1,192,1536]{2,1,0:T(8,128)S(1)} %copy-done.4, bf16[192,1536]{1,0:T(8,128)(2,1)} %get-tuple-element.11), kind=kLoop, calls=%fused_computation.9 | loop fusion | flops 4128768 | bytes 7667712 | tf_op jit(solution)/shard_map/broadcast_in_dim | solution.py:408
  75.4 0.0 copy-done
  75.4 1.7 %copy.14 = bf16[1,1024,1536]{2,1,0:T(8,128)(2,1)} copy(bf16[1,1024,1536]{2,1,0:T(8,128)(2,1)S(1)} %bitcast.22) | data formatting | bytes 6291456
Async XLA Ops:
  0.6 68.6 %copy-start.1 = (f32[192,384]{1,0:T(8,128)S(1)}, f32[192,384]{1,0:T(8,128)}, u32[]{:S(2)}) copy-start(f32[192,384]{1,0:T(8,128)} %anchor_hbm.1) | copy-start | bytes 884740
  0.6 68.6 %copy-start.2 = (f32[192,384]{1,0:T(8,128)S(1)}, f32[192,384]{1,0:T(8,128)}, u32[]{:S(2)}) copy-start(f32[192,384]{1,0:T(8,128)} %momentum_hbm.1) | copy-start | bytes 884740
  0.7 70.6 %copy-start.4 = (f32[1,192,1536]{2,1,0:T(8,128)S(1)}, f32[1,192,1536]{2,1,0:T(8,128)}, u32[]{:S(2)}) copy-start(f32[1,192,1536]{2,1,0:T(8,128)} %param.10) | copy-start | bytes 3538948
  69.2 2.0 %copy-start.3 = (f32[1,192,1536]{2,1,0:T(8,128)S(1)}, f32[1,192,1536]{2,1,0:T(8,128)}, u32[]{:S(2)}) copy-start(f32[1,192,1536]{2,1,0:T(8,128)} %param.11) | copy-start | bytes 3538948
  71.2 4.2 %copy-start = (bf16[1024,1536]{1,0:T(8,128)(2,1)S(1)}, bf16[1024,1536]{1,0:T(8,128)(2,1)}, u32[]{:S(2)}) copy-start(bf16[1024,1536]{1,0:T(8,128)(2,1)} %get-tuple-element.13) | copy-start | bytes 9437188

commit v3 on v2

--- a/solution.py
+++ b/solution.py
@@ -163,7 +163,7 @@
             own[i, :, here] = jnp.where(y == 0, upper, lower)
             psend[i, :, here] = jnp.where(y == 0, lower, upper).astype(bf16)
 
-            @pl.when(i < 2)
+            @pl.when(i < last)
             def _():
                 y_copy(i, h).start()
 
@@ -214,6 +214,37 @@
     pending.append(forward("x", ax_s, ax_r, 0, here, flip_x))
     pending.append(forward("s", as_s, as_r, 0, here, sibling))
 
+    lines = 16
+
+    def chain_copy(i):
+        slot, device = route(i)
+        return remote(zsend.at[i], chain.at[slot], ch_s.at[i], ch_r.at[slot], device)
+
+    def reduce_step(i, joins):
+        for h in range(2):
+            y_copy(i, h).wait_recv()
+        copy = chain_copy(i)
+        if joins:
+            copy.wait_recv()
+        slot, _ = route(i)
+
+        def add(j, carry):
+            there = pl.ds(pl.multiple_of(j * lines, lines), lines)
+            total = own[i, there] + ry[i, there].astype(f32)
+            if joins:
+                total = total + chain[slot, there].astype(f32)
+            zsend[i, there] = total.astype(bf16)
+            return carry
+
+        lax.fori_loop(0, rows // lines, add, 0)
+        copy.start()
+
+    outer = jnp.logical_not(inner)
+
+    @pl.when(outer)
+    def _():
+        reduce_step(0, False)
+
     @pl.when(inner)
     def _():
         def pass_on(i, carry):
@@ -232,49 +263,9 @@
         pending.append(forward("y", ay_s, ay_r, k, where, flip_y))
         pending.append(forward("x", ax_s, ax_r, k, where, flip_x))
         pending.append(forward("s", as_s, as_r, k, where, sibling))
-    for i in range(2, depth):
-        for h in range(2):
-            y_copy(i, h).start()
-
-    lines = 16
-
-    def reduce_step(i):
-        for h in range(2):
-            y_copy(i, h).wait_recv()
-        slot, device = route(i)
-        copy = remote(zsend.at[i], chain.at[slot], ch_s.at[i], ch_r.at[slot], device)
-
-        @pl.when(inner)
-        def _():
-            copy.wait_recv()
-
-            def add(j, carry):
-                there = pl.ds(pl.multiple_of(j * lines, lines), lines)
-                zsend[i, there] = (
-                    own[i, there] + ry[i, there].astype(f32) + chain[slot, there].astype(f32)
-                ).astype(bf16)
-                return carry
-
-            lax.fori_loop(0, rows // lines, add, 0)
-
-        @pl.when(jnp.logical_not(inner))
-        def _():
-            def add(j, carry):
-                there = pl.ds(pl.multiple_of(j * lines, lines), lines)
-                zsend[i, there] = (own[i, there] + ry[i, there].astype(f32)).astype(bf16)
-                return carry
-
-            lax.fori_loop(0, rows // lines, add, 0)
-
-        copy.start()
-        return copy
-
-    chains = [reduce_step(0)]
-    for k in range(depth):
-        where = ((z + depth - k) % depth, 1 - y, x, core)
-        arrived(ay_r, ay_s, k, where)
-        pending.append(forward("x", ax_s, ax_r, depth + k, where, flip_x))
-        pending.append(forward("s", as_s, as_r, depth + k, where, sibling))
+    for h in range(2):
+        y_copy(last, h).start()
+
     for slot, follows in ((z, z > 0), (depth + z, z < last)):
         @pl.when(follows)
         def _():
@@ -285,8 +276,27 @@
     lead_out[...] = lead_own[last, pl.ds(pl.multiple_of((1 - y) * rows, 8), rows)].astype(bf16)
     lead_swap = remote(lead_out, lead_in, ly_s.at[0], ly_r.at[0], flip_y)
     lead_swap.start()
-    for i in range(1, last):
-        chains.append(reduce_step(i))
+
+    @pl.when(outer)
+    def _():
+        for i in range(1, last):
+            reduce_step(i, False)
+
+    @pl.when(inner)
+    def _():
+        reduce_step(0, True)
+
+    for k in range(depth):
+        where = ((z + depth - k) % depth, 1 - y, x, core)
+        arrived(ay_r, ay_s, k, where)
+        pending.append(forward("x", ax_s, ax_r, depth + k, where, flip_x))
+        pending.append(forward("s", as_s, as_r, depth + k, where, sibling))
+
+    @pl.when(inner)
+    def _():
+        for i in range(1, last):
+            reduce_step(i, True)
+
     for dy in range(2):
         for k in range(depth):
             where = ((z + depth - k) % depth, y + dy - 2 * y * dy, 1 - x, core)
@@ -330,13 +340,14 @@
             ).wait_recv()
             grad_ref[:, lead:] += chain[slot].astype(f32) * scale
 
-    for copy in parts + pending + chains + [lead_swap]:
+    for copy in parts + pending + [lead_swap]:
         copy.wait_send()
     for i in range(depth):
         for h in range(2):
             y_copy(i, h).wait_send()
     for i in range(last):
         lead_copy(i).wait_send()
+        chain_copy(i).wait_send()
     for c in range(depth):
         back_copy(c).wait()
 

time: 78.3 us -> 78.3 us (level)
  no operation moved by 1% of the time
where the time goes in v3:
time: 78.3 us; the launch traced here: 77.3 us
  Pallas kernels  68.8 us (88%)
  other arithmetic  6.14 us (8%)
  local copies, waits for them, and re-layouts  1.69 us (2%)
    pallas_call x1, Pallas kernels, fused_shards(): pl.pallas_call(functools.partial(kernel, depth, groups, scale), out_shape...  68.8 us
    broadcast_in_dim x1, other arithmetic, fused_shards(): second[None]  4.2 us
    sub x1, other arithmetic, outer_step(): new_anchor = anchor - outer_rate * (outer_grad + outer_mu * new_momentum)  1.94 us
    unnamed x11, local copies, waits for them, and re-layouts  1.69 us

profile of v3, /device:TPU:0, one launch (start us, length us, event | category | flops | bytes accessed | tf_op | source)
XLA Modules:
  0.0 77.3 jit_solution(7772176267377714404)
XLA Ops:
  0.6 0.0 copy-start.1
  0.6 0.0 copy-start.2
  0.7 0.0 copy-start.4
  0.7 68.8 %shard_map.118 = (f32[192,384]{1,0:T(8,128)}, bf16[192,1536]{1,0:T(8,128)(2,1)}, f32[192,1536]{1,0:T(8,128)}, bf16[1024,1536]{1,0:T(8,128)(2,1)}) custom-call(f32[192,384]{1,0:T(8,128)} %anchor_hbm.1, f32[192,384]{1,0:T(8,128)} %momentum_hbm.1, f32[192,1536]{1,0:T(8,128)} %bitcast.25, bf16[1024,1536]{1,0:T(8,128)(2,1)} %bitcast.23, bf16[1024,1536]{1,0:T(8,128)(2,1)} %bitcast.24), custom_call_target="tpu_custom_call" | custom-call | tf_op jit(solution)/shard_map/pallas_call | solution.py:372
  69.5 0.0 copy-start.3
  69.5 0.0 copy-done.1
  69.5 0.0 copy-done.2
  69.5 1.9 %multiply_subtract_fusion = (f32[192,384]{1,0:T(8,128)}, f32[192,384]{1,0:T(8,128)}) fusion(f32[192,384]{1,0:T(8,128)S(1)} %copy-done.1, f32[192,384]{1,0:T(8,128)} %get-tuple-element.10, f32[192,384]{1,0:T(8,128)S(1)} %copy-done.2), kind=kLoop, calls=%fused_computation.10 | loop fusion | flops 589824 | bytes 1474560 | tf_op jit(solution)/shard_map/sub | solution.py:35
  71.4 0.0 copy-done.4
  71.4 0.0 copy-done.3
  71.4 0.0 copy-start
  71.4 4.2 %fusion.5 = (f32[1,192,1536]{2,1,0:T(8,128)}, f32[1,192,1536]{2,1,0:T(8,128)}, f32[1,192,1536]{2,1,0:T(8,128)}) fusion(f32[192,1536]{1,0:T(8,128)} %get-tuple-element.12, f32[1,192,1536]{2,1,0:T(8,128)S(1)} %copy-done.3, f32[1,192,1536]{2,1,0:T(8,128)S(1)} %copy-done.4, bf16[192,1536]{1,0:T(8,128)(2,1)} %get-tuple-element.11), kind=kLoop, calls=%fused_computation.9 | loop fusion | flops 4128768 | bytes 7667712 | tf_op jit(solution)/shard_map/broadcast_in_dim | solution.py:419
  75.6 0.0 copy-done
  75.6 1.7 %copy.14 = bf16[1,1024,1536]{2,1,0:T(8,128)(2,1)} copy(bf16[1,1024,1536]{2,1,0:T(8,128)(2,1)S(1)} %bitcast.22) | data formatting | bytes 6291456
Async XLA Ops:
  0.6 68.8 %copy-start.1 = (f32[192,384]{1,0:T(8,128)S(1)}, f32[192,384]{1,0:T(8,128)}, u32[]{:S(2)}) copy-start(f32[192,384]{1,0:T(8,128)} %anchor_hbm.1) | copy-start | bytes 884740
  0.6 68.8 %copy-start.2 = (f32[192,384]{1,0:T(8,128)S(1)}, f32[192,384]{1,0:T(8,128)}, u32[]{:S(2)}) copy-start(f32[192,384]{1,0:T(8,128)} %momentum_hbm.1) | copy-start | bytes 884740
  0.7 70.8 %copy-start.4 = (f32[1,192,1536]{2,1,0:T(8,128)S(1)}, f32[1,192,1536]{2,1,0:T(8,128)}, u32[]{:S(2)}) copy-start(f32[1,192,1536]{2,1,0:T(8,128)} %param.10) | copy-start | bytes 3538948
  69.5 2.0 %copy-start.3 = (f32[1,192,1536]{2,1,0:T(8,128)S(1)}, f32[1,192,1536]{2,1,0:T(8,128)}, u32[]{:S(2)}) copy-start(f32[1,192,1536]{2,1,0:T(8,128)} %param.11) | copy-start | bytes 3538948
  71.4 4.2 %copy-start = (bf16[1024,1536]{1,0:T(8,128)(2,1)S(1)}, bf16[1024,1536]{1,0:T(8,128)(2,1)}, u32[]{:S(2)}) copy-start(bf16[1024,1536]{1,0:T(8,128)(2,1)} %get-tuple-element.13) | copy-start | bytes 9437188
